TPU v7x, 32 devices: a whole 2x2x4 slice. The times are simulated.
32 devices in a mesh: island: 16 (over z, y, x), tensor: 2 (over core).
Axes of the slice: x: 2, y: 2, z: 4, core: 2. Of those that a mesh axis runs over, the one named last changes fastest.
Arguments:
- pseudo_grad: float32 [16, 32, 53248], P('island', None, 'tensor'), may hold values from -8000 to 8000
- outer_params: float32 [32, 53248], P('island', 'tensor'), may hold values from -4 to 4
- momentum: float32 [32, 53248], P('island', 'tensor'), may hold values from -6 to 6
- save_pages: int32 [16], replicated, may hold values from 1 to 832, 6656 in all
- writer: int32 [16], replicated, may hold values from 0 to 15, each once
Outputs:
- new_master: float32 [32, 53248], P('island', 'tensor')
- new_momentum: float32 [32, 53248], P('island', 'tensor')
- checkpoint: bfloat16 [16, 832, 256], P('island', None, 'tensor')
Inputs may be any that keep to these rules, and one draw needn't show every extreme that they name: save_pages sums to 6656; the longest range has exactly 832 pages. writer names every island once.
All inputs are finite; a program needn't handle non-finite values.
Results may differ from a plain program's by a relative error of at most 0.0007.
Values may be sent and summed in bfloat16 or wider, within the bound.
A program may use at most 64 MiB of HBM per device.

v0:
```python
import jax
import jax.numpy as jnp
from jax import lax
from jax.sharding import PartitionSpec as P

epsilon = 1e-06
decay_rate = 0.9
outer_rate = 0.7


def body(pseudo_grad, outer_params, momentum, save_pages, writer):
    own_rows = outer_params.shape[0]
    col_width = outer_params.shape[1]
    islands = lax.axis_size("island")
    my_index = lax.axis_index("island")
    own_grad = pseudo_grad[0]
    entries = own_grad.shape[0] * col_width * lax.axis_size("tensor")
    summed = lax.psum(own_grad, "island")
    full_grad = summed / islands
    square_sum = lax.psum(jnp.sum(full_grad * full_grad), "tensor")
    outer_grad = lax.dynamic_slice_in_dim(full_grad, my_index * own_rows, own_rows, 0)
    normed = outer_grad / jnp.sqrt(square_sum / entries + epsilon)
    new_momentum = decay_rate * momentum + normed
    new_master = outer_params - outer_rate * (normed + decay_rate * new_momentum)
    cast_rows = new_master.astype(jnp.bfloat16)
    pages_own = own_rows * col_width // 128
    capacity = 2 * pages_own
    starts = jnp.cumsum(save_pages) - save_pages
    targets = jnp.arange(islands, dtype=jnp.int32)
    owner_table = writer[None, :] == targets[:, None]
    range_start = jnp.sum(jnp.where(owner_table, starts[None, :], 0), axis=1)
    range_length = jnp.sum(jnp.where(owner_table, save_pages[None, :], 0), axis=1)
    is_mine = targets == my_index
    own_start = jnp.sum(jnp.where(is_mine, range_start, 0))
    own_length = jnp.sum(jnp.where(is_mine, range_length, 0))
    slot_ids = jnp.arange(capacity, dtype=jnp.int32)
    own_pages = cast_rows.reshape(pages_own, 128)
    spread_slots = -(-pages_own // islands)
    deliver_slots = -(-capacity // islands)
    spread_ids = jnp.arange(spread_slots, dtype=jnp.int32)
    offset = jnp.mod(targets - my_index * pages_own, islands)
    local_index = offset[:, None] + islands * spread_ids[None, :]
    live_slot = (local_index < pages_own).reshape(-1, 1)
    outgoing = jnp.take(own_pages, jnp.clip(local_index, 0, pages_own - 1).reshape(-1), axis=0)
    outgoing = jnp.where(live_slot, outgoing, jnp.zeros_like(outgoing))
    spread = lax.all_to_all(outgoing, "island", split_axis=0, concat_axis=0, tiled=True)
    deliver_ids = jnp.arange(deliver_slots, dtype=jnp.int32)
    first_page = range_start + jnp.mod(my_index - range_start, islands)
    global_page = first_page[:, None] + islands * deliver_ids[None, :]
    live_out = (global_page < (range_start + range_length)[:, None]).reshape(-1, 1)
    held_index = (
        global_page // pages_own * spread_slots + jnp.mod(global_page, pages_own) // islands
    )
    held_index = jnp.clip(held_index, 0, islands * spread_slots - 1).reshape(-1)
    forward = jnp.take(spread, held_index, axis=0)
    forward = jnp.where(live_out, forward, jnp.zeros_like(forward))
    delivered = lax.all_to_all(forward, "island", split_axis=0, concat_axis=0, tiled=True)
    source = jnp.mod(own_start + slot_ids, islands) * deliver_slots + slot_ids // islands
    source = jnp.clip(source, 0, islands * deliver_slots - 1)
    packed = jnp.take(delivered, source, axis=0)
    packed = jnp.where((slot_ids < own_length)[:, None], packed, jnp.zeros_like(packed))
    return (new_master, new_momentum, packed[None])


def solution(mesh):
    in_specs = (P("island", None, "tensor"), P("island", "tensor"), P("island", "tensor"), P(), P())
    out_specs = (P("island", "tensor"), P("island", "tensor"), P("island", None, "tensor"))
    return jax.shard_map(body, mesh=mesh, in_specs=in_specs, out_specs=out_specs, check_vma=False)
```

profile of v0, /device:TPU:0, one launch (start us, length us, event | category | flops | bytes accessed | tf_op | source)
XLA Modules:
  0.0 218.6 jit_solution(9376555139836277744)
XLA Ops:
  7.2 0.0 copy-start
  7.2 0.0 copy-start.1
  7.2 0.0 all-reduce.2.cloned.1.call-start
  7.2 0.7 all-reduce.2.cloned.1.call-update
  8.0 0.1 add_clamp_fusion
  8.0 0.1 min.40
  8.1 0.0 copy-done
  8.1 0.1 copy.10
  8.3 0.1 reduce
  8.4 0.0 copy-done.1
  8.4 0.1 select_reduce_fusion.1
  8.5 0.7 fusion.32
  9.2 0.1 add_divide_fusion
  9.3 0.1 rem.175
  9.4 0.1 div.75
  9.5 0.1 add_compare_fusion
  9.6 0.1 ne.202
  9.7 0.1 add_compare_fusion.1
  9.8 159.0 %all-reduce.2.cloned.1.call-done = f32[32,26624]{1,0:T(8,128)} async-done(((f32[32,26624]{1,0:T(8,128)}), f32[32,26624]{1,0:T(8,128)}) %all-reduce.2.cloned.1.call-update) | async-done | bytes 3407888 | tf_op jit(solution)/shard_map/psum | solution.py:18
  168.8 3.5 %broadcast_multiply_fusion = (f32[32,26624]{1,0:T(8,128)S(1)}, f32[]{:T(128)}) fusion(f32[32,26624]{1,0:T(8,128)} %all-reduce.2.cloned.1.call-done), kind=kLoop, calls=%fused_computation.4 | loop fusion | flops 2555903 | bytes 6815748 | tf_op jit(solution)/shard_map/div | solution.py:19
  172.2 3.1 %psum.15 = f32[]{:T(128)} all-reduce(f32[]{:T(128)} %get-tuple-element.9), channel_id=1, replica_groups=mesh['island'=16,'tensor'=2] {'tensor'}, use_global_device_ids=true, to_apply=%region_2.0 | all-reduce | flops 1 | bytes 8 | tf_op jit(solution)/shard_map/psum | solution.py:20
  176.0 2.1 fusion.36
  178.1 0.1 reshape.458
  178.2 1.5 gather_fusion
  179.7 0.9 select_select_fusion.1
  180.6 4.7 %all-to-all-start = ((bf16[16,26,128]{2,1,0:T(8,128)(2,1)}), bf16[16,26,128]{2,1,0:T(8,128)(2,1)S(1)}, u32[]{:S(2)}, u32[]{:S(2)}) async-start(bf16[16,26,128]{2,1,0:T(8,128)(2,1)} %select_select_fusion.1), calls=%async_computation | async-start | bytes 262144 | tf_op jit(solution)/shard_map/all_to_all | solution.py:46
  185.3 0.1 fusion.25
  185.4 7.7 %all-to-all-done = bf16[16,26,128]{2,1,0:T(8,128)(2,1)S(1)} async-done(((bf16[16,26,128]{2,1,0:T(8,128)(2,1)}), bf16[16,26,128]{2,1,0:T(8,128)(2,1)S(1)}, u32[]{:S(2)}, u32[]{:S(2)}) %all-to-all-start) | async-done | bytes 106528 | tf_op jit(solution)/shard_map/all_to_all | solution.py:46
  193.1 2.4 %gather_fusion.1 = bf16[832,128]{1,0:T(8,128)(2,1)S(1)} fusion(bf16[416,128]{1,0:T(8,128)(2,1)S(1)} %all_to_all.13, s32[1024]{0:T(1024)S(1)} %pad_clamp_fusion.1), kind=kCustom, calls=%fused_computation.1 | custom fusion | bytes 429312 | tf_op jit(solution)/shard_map/jit(_take)/gather | solution.py:55
  195.5 1.0 select_select_fusion
  196.5 3.5 %all-to-all-start.1 = ((bf16[16,52,128]{2,1,0:T(8,128)(2,1)}), bf16[16,52,128]{2,1,0:T(8,128)(2,1)S(1)}, u32[]{:S(2)}, u32[]{:S(2)}) async-start(bf16[16,52,128]{2,1,0:T(8,128)(2,1)} %select_select_fusion), calls=%async_computation.1 | async-start | bytes 458752 | tf_op jit(solution)/shard_map/all_to_all | solution.py:57
  200.1 0.7 fusion.26
  200.8 1.3 iota_compare_fusion.1
  202.1 6.3 %all-to-all-done.1 = bf16[16,52,128]{2,1,0:T(8,128)(2,1)S(1)} async-done(((bf16[16,52,128]{2,1,0:T(8,128)(2,1)}), bf16[16,52,128]{2,1,0:T(8,128)(2,1)S(1)}, u32[]{:S(2)}, u32[]{:S(2)}) %all-to-all-start.1) | async-done | bytes 213024 | tf_op jit(solution)/shard_map/all_to_all | solution.py:57
  208.4 2.4 %gather_fusion.2 = bf16[832,128]{1,0:T(8,128)(2,1)S(1)} fusion(bf16[832,128]{1,0:T(8,128)(2,1)S(1)} %all_to_all.15, s32[1024]{0:T(1024)S(1)} %pad_clamp_fusion), kind=kCustom, calls=%fused_computation.2 | custom fusion | bytes 429312 | tf_op jit(solution)/shard_map/jit(_take)/gather | solution.py:60
  210.8 1.0 fusion
  (13 shorter events, 0.2 us)
Async XLA Ops:
  7.2 1.0 copy-start
  7.2 1.2 copy-start.1
  7.2 161.6 %all-reduce.2.cloned.1.call-start = ((), (), s32[]{:S(2)}) async-start(), calls=%async_computation.2 | async-start | bytes 6815744 | tf_op jit(solution)/shard_map/psum | solution.py:18
  180.6 12.5 %all-to-all-start = ((bf16[16,26,128]{2,1,0:T(8,128)(2,1)}), bf16[16,26,128]{2,1,0:T(8,128)(2,1)S(1)}, u32[]{:S(2)}, u32[]{:S(2)}) async-start(bf16[16,26,128]{2,1,0:T(8,128)(2,1)} %select_select_fusion.1), calls=%async_computation | async-start | bytes 262144 | tf_op jit(solution)/shard_map/all_to_all | solution.py:46
  196.5 11.8 %all-to-all-start.1 = ((bf16[16,52,128]{2,1,0:T(8,128)(2,1)}), bf16[16,52,128]{2,1,0:T(8,128)(2,1)S(1)}, u32[]{:S(2)}, u32[]{:S(2)}) async-start(bf16[16,52,128]{2,1,0:T(8,128)(2,1)} %select_select_fusion), calls=%async_computation.1 | async-start | bytes 458752 | tf_op jit(solution)/shard_map/all_to_all | solution.py:57
Sparse Core Ops, SparseCore 0:
  13.7 155.0 all-reduce.1
where the time goes:
time: 219 us
  waiting for transfers between devices  174 us (79%)
  between operations  14.9 us (7%)
  other arithmetic  11.8 us (5%)
  starting transfers between devices  8.25 us (4%)
  local copies, waits for them, and re-layouts  6.87 us (3%)
  blocking collectives  3.08 us (1%)
    psum x1, waiting for transfers between devices, body(): summed = lax.psum(own_grad, 'island')  159 us
    all_to_all x1, waiting for transfers between devices, body(): lax.all_to_all(outgoing, 'island', split_axis=0, concat_axis=0, tiled=True)  7.72 us
    all_to_all x1, waiting for transfers between devices, body(): lax.all_to_all(forward, 'island', split_axis=0, concat_axis=0, tiled=True)  6.3 us
    all_to_all x1, starting transfers between devices, body(): lax.all_to_all(outgoing, 'island', split_axis=0, concat_axis=0, tiled=True)  4.69 us
  transfers between devices with their start and end apart: 3, of which 3 were waited for; matrix products, arithmetic and copies ran while one was open for 2% of the time, Pallas kernels for 0%

commit v1 on v0

v1 whole, which is shorter than its diff:
```python
import functools

import jax
import jax.numpy as jnp
from jax import lax
from jax.experimental import pallas as pl
from jax.experimental.pallas import tpu as pltpu
from jax.sharding import PartitionSpec as P

epsilon = 1e-06
decay_rate = 0.9
outer_rate = 0.7
LANES = 128
ROUNDS = 3
GATHER_ROUNDS = 2
MESH = pl.DeviceIdType.MESH


def cuts(total, unit, count):
    units = -(-total // unit)
    count = min(count, units)
    edges = [min(total, unit * (units * i // count)) for i in range(count + 1)]
    return [(edges[i], edges[i + 1] - edges[i]) for i in range(count)]


def bit_orders(bits):
    base = list(range(bits))
    orders = []
    for lead in range(min(3, bits)):
        orders.append([lead] + [b for b in base if b != lead])
    return orders


def at(bits_left, fixed, span):
    return tuple(fixed.get(b, slice(None)) for b in bits_left) + (pl.ds(*span), slice(None))


def kernel(bits, tensor, entries, x_ref, par_ref, mom_ref, master_ref, moment_ref, pages_ref, *scratch):
    acc = [x_ref] + list(scratch[:bits])
    sums, gathered, hi_sq, lo_sq = scratch[bits : bits + 4]
    rs_send, rs_recv, ag_send, ag_recv, hi_send, hi_recv, lo_send, lo_recv, out_sem = scratch[bits + 4 :]
    page_count = par_ref.shape[0]
    islands = 1 << bits
    me = lax.axis_index("island")
    my_t = lax.axis_index("tensor")
    mine = [lax.rem(me // (1 << b), 2) for b in range(bits)]
    partner = [me + (1 - 2 * mine[b]) * (1 << b) for b in range(bits)]
    all_bits = list(range(bits - 1, -1, -1))
    low_bits = bits // 2
    n_lo, n_hi = 1 << low_bits, 1 << (bits - low_bits)

    def flip(value, mask, width):
        out = value
        for b in range(width):
            if mask >> b & 1:
                out = out + (1 - 2 * lax.rem(value // (1 << b), 2)) * (1 << b)
        return out

    hi_peers = [(k, {"island": flip(me, k * n_lo, bits)}) for k in range(1, n_hi)]
    t_bits = tensor.bit_length() - 1
    lo_peers = []
    for k in range(1, n_lo * tensor):
        k_lo, k_t = k // tensor, k % tensor
        lo_peers.append((k, {"island": flip(me, k_lo, bits), "tensor": flip(my_t, k_t, t_bits)}))

    barrier = pltpu.get_barrier_semaphore()
    for _, peer in hi_peers + lo_peers:
        pl.semaphore_signal(barrier, inc=1, device_id=peer, device_id_type=MESH)
    pl.semaphore_wait(barrier, len(hi_peers) + len(lo_peers))

    orders = bit_orders(bits)
    spans = cuts(page_count, 8, len(orders) * ROUNDS)

    def left(c, s):
        used = orders[c % len(orders)][:s]
        return [b for b in all_bits if b not in used]

    def rs_copy(c, s):
        d = orders[c % len(orders)][s - 1]
        return pltpu.make_async_remote_copy(
            src_ref=acc[s - 1].at[at(left(c, s - 1), {d: 1 - mine[d]}, spans[c])],
            dst_ref=acc[s].at[at(left(c, s), {}, spans[c])],
            send_sem=rs_send.at[c, s - 1],
            recv_sem=rs_recv.at[c, s - 1],
            device_id={"island": partner[d]},
            device_id_type=MESH,
        )

    copies = {}
    for c in range(len(spans)):
        copies[c, 1] = rs_copy(c, 1)
        copies[c, 1].start()

    def when(item):
        c, s = item
        r = c // len(orders)
        return (0.1 * r if s == 1 else 1.1 * s + r, c)

    steps = sorted(((c, s) for c in range(len(spans)) for s in range(1, bits + 1)), key=when)
    for c, s in steps:
        order = orders[c % len(orders)]
        d = order[s - 1]
        copies[c, s].wait_recv()
        if s == bits:
            total = acc[s][at([], {}, spans[c])] + acc[s - 1][at(left(c, s - 1), {d: mine[d]}, spans[c])]
            sums[pl.ds(*spans[c]), :] = total * (1.0 / islands)
            continue
        e = order[s]
        for side in (1 - mine[e], mine[e]):
            to = at(left(c, s), {e: side}, spans[c])
            of = at(left(c, s - 1), {d: mine[d], e: side}, spans[c])
            acc[s][to] = acc[s][to] + acc[s - 1][of]
            if (c, s + 1) not in copies:
                copies[c, s + 1] = rs_copy(c, s + 1)
                copies[c, s + 1].start()

    grad = sums[...]
    hi_sq[0] = jnp.sum((grad * grad).reshape(page_count // 8, 8, LANES), axis=0)

    def exchange(box, peers, send, recv):
        sent = []
        for k, peer in peers:
            copy = pltpu.make_async_remote_copy(
                src_ref=box.at[0],
                dst_ref=box.at[k],
                send_sem=send.at[k],
                recv_sem=recv.at[k],
                device_id=peer,
                device_id_type=MESH,
            )
            copy.start()
            sent.append(copy)
        for copy in sent:
            copy.wait_recv()
        return sent

    sent = exchange(hi_sq, hi_peers, hi_send, hi_recv)
    lo_sq[0] = jnp.sum(hi_sq[...], axis=0)
    sent += exchange(lo_sq, lo_peers, lo_send, lo_recv)
    square_sum = jnp.sum(jnp.sum(lo_sq[...], axis=0), keepdims=True)
    norm = jnp.sqrt(square_sum / entries + epsilon)
    normed = grad / norm
    moment = decay_rate * mom_ref[...] + normed
    master = par_ref[...] - outer_rate * (normed + decay_rate * moment)
    gathered[tuple(mine[b] for b in all_bits)] = master.astype(jnp.bfloat16)

    ag_spans = cuts(page_count, 16, len(orders) * GATHER_ROUNDS)

    def ag_copy(c, s):
        order = orders[c % len(orders)][::-1]
        held = order[:s]
        where = at(all_bits, {b: mine[b] for b in all_bits if b not in held}, ag_spans[c])
        return pltpu.make_async_remote_copy(
            src_ref=gathered.at[where],
            dst_ref=gathered.at[where],
            send_sem=ag_send.at[c, s],
            recv_sem=ag_recv.at[c, s],
            device_id={"island": partner[order[s]]},
            device_id_type=MESH,
        )

    ag = {}
    for c in range(len(ag_spans)):
        ag[c, 0] = ag_copy(c, 0)
        ag[c, 0].start()
    moment_ref[...] = moment
    master_ref[...] = master
    for s in range(bits):
        for c in range(len(ag_spans)):
            ag[c, s].wait_recv()
            if s + 1 < bits:
                ag[c, s + 1] = ag_copy(c, s + 1)
                ag[c, s + 1].start()

    outs = []
    for i in range(islands):
        copy = pltpu.make_async_copy(
            gathered.at[tuple(i >> b & 1 for b in all_bits)], pages_ref.at[i], out_sem.at[i]
        )
        copy.start()
        outs.append(copy)
    for copy in list(copies.values()) + list(ag.values()) + sent:
        copy.wait_send()
    for copy in outs:
        copy.wait()


def body(islands, tensor, pseudo_grad, outer_params, momentum, save_pages, writer):
    own_rows, col_width = outer_params.shape
    bits = islands.bit_length() - 1
    page_count = own_rows * col_width // LANES
    capacity = 2 * page_count
    my_index = lax.axis_index("island")
    entries = islands * own_rows * col_width * tensor
    x = pseudo_grad.reshape((2,) * bits + (page_count, LANES))
    f32, bf16 = jnp.float32, jnp.bfloat16
    orders = len(bit_orders(bits))
    n_rs = len(cuts(page_count, 8, orders * ROUNDS))
    n_ag = len(cuts(page_count, 16, orders * GATHER_ROUNDS))
    n_lo = 1 << (bits // 2)
    n_hi = islands // n_lo
    dma = pltpu.SemaphoreType.DMA
    vmem = pl.BlockSpec(memory_space=pltpu.VMEM)
    spare = -(-capacity // page_count)
    master, moment, pages = pl.pallas_call(
        functools.partial(kernel, bits, tensor, entries),
        out_shape=(
            jax.ShapeDtypeStruct((page_count, LANES), f32),
            jax.ShapeDtypeStruct((page_count, LANES), f32),
            jax.ShapeDtypeStruct((islands + spare, page_count, LANES), bf16),
        ),
        in_specs=[vmem] * 3,
        out_specs=(vmem, vmem, pl.BlockSpec(memory_space=pl.ANY)),
        scratch_shapes=[pltpu.VMEM((2,) * (bits - s) + (page_count, LANES), f32) for s in range(1, bits + 1)]
        + [
            pltpu.VMEM((page_count, LANES), f32),
            pltpu.VMEM((2,) * bits + (page_count, LANES), bf16),
            pltpu.VMEM((n_hi, 8, LANES), f32),
            pltpu.VMEM((n_lo * tensor, 8, LANES), f32),
            dma((n_rs, bits)),
            dma((n_rs, bits)),
            dma((n_ag, bits)),
            dma((n_ag, bits)),
            dma((n_hi,)),
            dma((n_hi,)),
            dma((n_lo * tensor,)),
            dma((n_lo * tensor,)),
            dma((islands,)),
        ],
        compiler_params=pltpu.CompilerParams(collective_id=0, has_side_effects=True),
    )(x, outer_params.reshape(page_count, LANES), momentum.reshape(page_count, LANES))

    starts = jnp.cumsum(save_pages) - save_pages
    is_mine = writer == my_index
    own_start = jnp.sum(jnp.where(is_mine, starts, 0))
    own_length = jnp.sum(jnp.where(is_mine, save_pages, 0))
    pages = pages.reshape(-1, LANES)
    window = lax.dynamic_slice_in_dim(pages, own_start, capacity, 0)
    live = jnp.arange(capacity, dtype=jnp.int32) < own_length
    packed = jnp.where(live[:, None], window, jnp.zeros_like(window))
    shape = (own_rows, col_width)
    return master.reshape(shape), moment.reshape(shape), packed[None]


def solution(mesh):
    in_specs = (P("island", None, "tensor"), P("island", "tensor"), P("island", "tensor"), P(), P())
    out_specs = (P("island", "tensor"), P("island", "tensor"), P("island", None, "tensor"))
    step = functools.partial(body, mesh.shape["island"], mesh.shape["tensor"])
    return jax.shard_map(step, mesh=mesh, in_specs=in_specs, out_specs=out_specs, check_vma=False)
```

time: 219 us -> 87.8 us (0.40)
  waiting for transfers between devices: 174 us -> 0 us
  Pallas kernels: 0 us -> 72.7 us
  between operations: 14.9 us -> 2.75 us
  other arithmetic: 11.8 us -> 3.33 us
  starting transfers between devices: 8.25 us -> 0 us
  blocking collectives: 3.08 us -> 0 us
    psum x1 -> x0, waiting for transfers between devices: 159 us -> none  [body(): summed = lax.psum(own_grad, 'island')]
    pallas_call x0 -> x1, Pallas kernels: none -> 72.7 us  [body(): pl.pallas_call(functools.partial(kernel, bits, tensor, entries), out_shap...]
    all_to_all x2 -> x0, waiting for transfers between devices: 14 us -> none  [the longest x1 7.72 us: body(): lax.all_to_all(outgoing, 'island', split_axis=0, concat_axis=0, tiled=True)]
    reshape x1 -> x5, local copies, waits for them, and re-layouts: 0.07 us -> 8.69 us  [the longest x2 3.49 us: body(): return (master.reshape(shape), moment.reshape(shape), packed[None])]
    all_to_all x2 -> x0, starting transfers between devices: 8.21 us -> none  [the longest x1 4.69 us: body(): lax.all_to_all(outgoing, 'island', split_axis=0, concat_axis=0, tiled=True)]
    gather x5 -> x0, local copies, waits for them, and re-layouts: 6.26 us -> none  [the longest x2 2.4 us: body(): forward = jnp.take(spread, held_index, axis=0)]
    select_n x7 -> x0, other arithmetic: 3.62 us -> none  [the longest x1 0.98 us: body(): forward = jnp.where(live_out, forward, jnp.zeros_like(forward))]
    div x2 -> x0, other arithmetic: 3.54 us -> none  [the longest x1 3.46 us: body(): full_grad = summed / islands]
  transfers between devices with their start and end apart: 3 -> 0, of which waited for: 3 -> 0; matrix products, arithmetic and copies ran while one was open for 2% -> 0% of each run, Pallas kernels for 0% -> 0%
where the time goes in v1:
time: 87.8 us; the launch traced here: 87.5 us
  Pallas kernels  72.7 us (83%)
  local copies, waits for them, and re-layouts  8.78 us (10%)
  other arithmetic  3.33 us (4%)
  between operations  2.75 us (3%)
    pallas_call x1, Pallas kernels, body(): pl.pallas_call(functools.partial(kernel, bits, tensor, entries), out_shap...  72.7 us
    reshape x2, local copies, waits for them, and re-layouts, body(): return (master.reshape(shape), moment.reshape(shape), packed[None])  3.49 us
    reshape x1, local copies, waits for them, and re-layouts, body(): x = pseudo_grad.reshape((2,) * bits + (page_count, LANES))  3.48 us
    broadcast_in_dim x1, other arithmetic, body(): return (master.reshape(shape), moment.reshape(shape), packed[None])  1.81 us

profile of v1, /device:TPU:0, one launch (start us, length us, event | category | flops | bytes accessed | tf_op | source)
XLA Modules:
  0.0 87.5 jit_solution(12899391934601763944)
XLA Ops:
  0.6 0.0 copy-start
  0.6 0.0 copy-start.1
  0.7 3.5 %reshape.54.x_ref = f32[2,2,2,2,416,128]{5,4,3,2,1,0:T(8,128)} reshape(f32[1,32,26624]{2,1,0:T(8,128)} %param.5) | data formatting | bytes 6815744 | tf_op jit(solution)/shard_map/reshape | solution.py:195
  4.1 0.0 copy-done
  4.1 0.0 copy-start.2
  4.1 0.0 copy-start.3
  4.1 0.9 reshape.55.par_ref
  5.0 0.0 copy-done.1
  5.0 0.9 reshape.56.mom_ref
  5.9 72.7 %shard_map.76 = (f32[416,128]{1,0:T(8,128)}, f32[416,128]{1,0:T(8,128)}, bf16[18,416,128]{2,1,0:T(8,128)(2,1)}) custom-call(f32[2,2,2,2,416,128]{5,4,3,2,1,0:T(8,128)} %reshape.54.x_ref, f32[416,128]{1,0:T(8,128)} %reshape.55.par_ref, f32[416,128]{1,0:T(8,128)} %reshape.56.mom_ref), custom_call_target="tpu_custom_call" | custom-call | tf_op jit(solution)/shard_map/pallas_call | solution.py:205
  78.5 1.7 %reshape.57 = f32[2,26624]{1,0:T(2,128)} reshape(f32[416,128]{1,0:T(8,128)} %get-tuple-element.6) | data formatting | bytes 425984 | tf_op jit(solution)/shard_map/reshape | solution.py:242
  80.3 1.7 %reshape.58 = f32[2,26624]{1,0:T(2,128)} reshape(f32[416,128]{1,0:T(8,128)} %get-tuple-element.7) | data formatting | bytes 425984 | tf_op jit(solution)/shard_map/reshape | solution.py:242
  82.0 0.0 copy-done.2
  82.0 0.1 copy.9
  82.1 0.1 reduce
  82.3 0.0 copy-done.3
  82.3 0.7 fusion
  85.1 0.7 iota_compare_fusion
  85.7 1.8 %select_bitcast_fusion = bf16[1,832,128]{2,1,0:T(8,128)(2,1)} fusion(bf16[7488,128]{1,0:T(8,128)(2,1)} %bitcast.4, s32[]{:T(128)S(6)} %select_n.16, pred[832]{0:T(1024)(128)(4,1)S(1)} %iota_compare_fusion), kind=kLoop, calls=%fused_computation | loop fusion | flops 106496 | bytes 426820 | tf_op jit(solution)/shard_map/broadcast_in_dim | solution.py:242
  (1 shorter events, 0.0 us)
Async XLA Ops:
  0.6 3.5 %copy-start = (f32[2,26624]{1,0:T(2,128)S(1)}, f32[2,26624]{1,0:T(2,128)}, u32[]{:S(2)}) copy-start(f32[2,26624]{1,0:T(2,128)} %param.6) | copy-start | bytes 638980
  0.6 4.4 %copy-start.1 = (f32[2,26624]{1,0:T(2,128)S(1)}, f32[2,26624]{1,0:T(2,128)}, u32[]{:S(2)}) copy-start(f32[2,26624]{1,0:T(2,128)} %param.7) | copy-start | bytes 638980
  4.1 77.9 %copy-start.2 = (s32[16]{0:T(128)S(1)}, s32[16]{0:T(128)}, u32[]{:S(2)}) copy-start(s32[16]{0:T(128)} %param.8) | copy-start | bytes 196
  4.1 78.1 %copy-start.3 = (s32[16]{0:T(128)S(1)}, s32[16]{0:T(128)}, u32[]{:S(2)}) copy-start(s32[16]{0:T(128)} %param.9) | copy-start | bytes 196

commit v2 on v1

v2 whole, which is shorter than its diff:
```python
import functools

import jax
import jax.numpy as jnp
from jax import lax
from jax.experimental import pallas as pl
from jax.experimental.pallas import tpu as pltpu
from jax.sharding import PartitionSpec as P

epsilon = 1e-06
decay_rate = 0.9
outer_rate = 0.7
LANES = 128
SUBLANES = 8
ROUNDS = 3
GATHER_CHUNKS = 2
MESH = pl.DeviceIdType.MESH


def cuts(total, unit, count):
    units = -(-total // unit)
    count = min(count, units)
    edges = [min(total, unit * (units * i // count)) for i in range(count + 1)]
    return [(edges[i], edges[i + 1] - edges[i]) for i in range(count)]


def bit_orders(bits):
    base = list(range(bits))
    orders = []
    for lead in range(min(3, bits)):
        orders.append([lead] + [b for b in base if b != lead])
    return orders


def at(bits_left, fixed, span):
    return tuple(fixed.get(b, slice(None)) for b in bits_left) + (pl.ds(*span), slice(None))


def flip(value, mask, width):
    out = value
    for b in range(width):
        if mask >> b & 1:
            out = out + (1 - 2 * lax.rem(value // (1 << b), 2)) * (1 << b)
    return out


def kernel(bits, tensor, rows, entries, *refs):
    x_ref, par_ref, mom_ref, save_ref, writer_ref, master_ref, moment_ref, pack_ref = refs[:8]
    scratch = refs[8:]
    page_count = par_ref.shape[0]
    capacity = pack_ref.shape[0]
    g_spans = cuts(page_count, 16, GATHER_CHUNKS)
    n_g = len(g_spans)
    acc = [x_ref] + list(scratch[:bits])
    held, parcel, landed = (scratch[bits + i * n_g : bits + (i + 1) * n_g] for i in range(3))
    scratch = scratch[bits + 3 * n_g :]
    sums, flat, span_buf, squares = scratch[:4]
    rs_send, rs_recv, sq_send, sq_recv, line_send, line_recv, del_send, del_recv = scratch[4:]
    islands = 1 << bits
    me = lax.axis_index("island")
    my_t = lax.axis_index("tensor")
    mine = [lax.rem(me // (1 << b), 2) for b in range(bits)]
    partner = [me + (1 - 2 * mine[b]) * (1 << b) for b in range(bits)]
    all_bits = list(range(bits - 1, -1, -1))
    n_lo = 1 << (bits // 2)
    n_hi = islands // n_lo
    my_hi, my_lo = me // n_lo, lax.rem(me, n_lo)

    t_bits = tensor.bit_length() - 1
    peers = []
    for k in range(1, islands * tensor):
        peers.append((k, {"island": flip(me, k // tensor, bits), "tensor": flip(my_t, k % tensor, t_bits)}))

    barrier = pltpu.get_barrier_semaphore()
    for _, peer in peers:
        pl.semaphore_signal(barrier, inc=1, device_id=peer, device_id_type=MESH)
    pl.semaphore_wait(barrier, len(peers))

    orders = bit_orders(bits)
    spans = cuts(page_count, 8, len(orders) * ROUNDS)

    def left(c, s):
        used = orders[c % len(orders)][:s]
        return [b for b in all_bits if b not in used]

    def rs_copy(c, s):
        d = orders[c % len(orders)][s - 1]
        return pltpu.make_async_remote_copy(
            src_ref=acc[s - 1].at[at(left(c, s - 1), {d: 1 - mine[d]}, spans[c])],
            dst_ref=acc[s].at[at(left(c, s), {}, spans[c])],
            send_sem=rs_send.at[c, s - 1],
            recv_sem=rs_recv.at[c, s - 1],
            device_id={"island": partner[d]},
            device_id_type=MESH,
        )

    copies = {}
    for c in range(len(spans)):
        copies[c, 1] = rs_copy(c, 1)
        copies[c, 1].start()

    def when(item):
        c, s = item
        r = c // len(orders)
        return (0.1 * r if s == 1 else 1.1 * s + r, c)

    steps = sorted(((c, s) for c in range(len(spans)) for s in range(1, bits + 1)), key=when)
    for c, s in steps:
        order = orders[c % len(orders)]
        d = order[s - 1]
        copies[c, s].wait_recv()
        if s == bits:
            total = acc[s][at([], {}, spans[c])] + acc[s - 1][at(left(c, s - 1), {d: mine[d]}, spans[c])]
            sums[pl.ds(*spans[c]), :] = total * (1.0 / islands)
            continue
        e = order[s]
        for side in (1 - mine[e], mine[e]):
            to = at(left(c, s), {e: side}, spans[c])
            of = at(left(c, s - 1), {d: mine[d], e: side}, spans[c])
            acc[s][to] = acc[s][to] + acc[s - 1][of]
            if (c, s + 1) not in copies:
                copies[c, s + 1] = rs_copy(c, s + 1)
                copies[c, s + 1].start()

    starts, running = [], jnp.int32(0)
    for k in range(islands):
        starts.append(running)
        running = running + save_ref[k]

    def range_of(island):
        start, length = jnp.int32(0), jnp.int32(0)
        for k in range(islands):
            hit = writer_ref[k] == island
            start = start + jnp.where(hit, starts[k], 0)
            length = length + jnp.where(hit, save_ref[k], 0)
        return start, length

    wanted = [range_of(flip(me, k, bits)) for k in range(n_lo)]
    first_block = [lax.div(start, jnp.int32(page_count)) for start, _ in wanted]

    grad = sums[...]
    squares[0] = jnp.sum((grad * grad).reshape(page_count // 8, 8, LANES), axis=0)
    sent = []
    for k, peer in peers:
        copy = pltpu.make_async_remote_copy(
            src_ref=squares.at[0],
            dst_ref=squares.at[k],
            send_sem=sq_send.at[k],
            recv_sem=sq_recv.at[k],
            device_id=peer,
            device_id_type=MESH,
        )
        copy.start()
        sent.append(copy)
    for copy in sent:
        copy.wait_recv()
    square_sum = jnp.sum(jnp.sum(squares[...], axis=0), keepdims=True)
    norm = jnp.sqrt(square_sum / entries + epsilon)
    normed = grad / norm
    moment = decay_rate * mom_ref[...] + normed
    master = par_ref[...] - outer_rate * (normed + decay_rate * moment)
    master_ref[...] = master
    moment_ref[...] = moment
    tiles = page_count // rows
    for r in range(rows):
        flat[pl.ds(r * tiles, tiles), :] = master_ref[pl.ds(r, tiles, stride=rows), :]
    for g, span in enumerate(g_spans):
        held[g][my_hi] = flat[pl.ds(*span), :].astype(jnp.bfloat16)

    def line(g, way, step):
        block = my_hi - step if way == 0 else my_hi + step
        return pltpu.make_async_remote_copy(
            src_ref=held[g].at[block],
            dst_ref=held[g].at[block],
            send_sem=line_send.at[g, way, step],
            recv_sem=line_recv.at[g, way, step],
            device_id={"island": me + n_lo if way == 0 else me - n_lo},
            device_id_type=MESH,
        )

    def sends(way, step):
        if way == 0:
            return jnp.logical_and(my_hi >= step, my_hi < n_hi - 1)
        return jnp.logical_and(my_hi <= n_hi - 1 - step, my_hi > 0)

    def arrives(way, step):
        return my_hi > step if way == 0 else my_hi < n_hi - 1 - step

    def start_line(g, way, step):
        pl.when(sends(way, step))(lambda: line(g, way, step).start())

    def end_line(g, way, step):
        def wait():
            block = my_hi - 1 - step if way == 0 else my_hi + 1 + step
            pltpu.make_async_remote_copy(
                src_ref=held[g].at[block],
                dst_ref=held[g].at[block],
                send_sem=line_send.at[g, way, step],
                recv_sem=line_recv.at[g, way, step],
                device_id={"island": me},
                device_id_type=MESH,
            ).wait_recv()

        pl.when(arrives(way, step))(wait)

    for g in range(n_g):
        for way in range(2):
            start_line(g, way, 0)
    parcels = []
    for g in range(n_g):
        for step in range(n_hi - 1):
            for way in range(2):
                end_line(g, way, step)
                if step + 1 < n_hi - 1:
                    start_line(g, way, step + 1)
        for k in range(n_lo - 1, -1, -1):
            ahead = lax.rem(my_lo + islands - first_block[k], jnp.int32(n_lo))
            which = lax.div(jnp.minimum(first_block[k] + ahead, islands - 1), jnp.int32(n_lo))
            if k == 0:
                landed[g][0] = held[g][which]
                continue
            parcel[g][k] = held[g][which]
            copy = pltpu.make_async_remote_copy(
                src_ref=parcel[g].at[k],
                dst_ref=landed[g].at[k],
                send_sem=del_send.at[g, k],
                recv_sem=del_recv.at[g, k],
                device_id={"island": flip(me, k, bits)},
                device_id_type=MESH,
            )
            copy.start()
            parcels.append(copy)
    spread = span_buf.shape[0] // page_count
    for g, (low, size) in enumerate(g_spans):
        for copy in parcels[g * (n_lo - 1) : (g + 1) * (n_lo - 1)]:
            copy.wait_recv()
        for m in range(spread):
            slot = lax.rem(first_block[0] + m, jnp.int32(n_lo)) ^ my_lo
            span_buf[pl.ds(m * page_count + low, size), :] = landed[g][slot].astype(jnp.float32)
    start, length = wanted[0]
    window = span_buf[pl.ds(start - first_block[0] * page_count, capacity), :]
    live = lax.broadcasted_iota(jnp.int32, window.shape, 0) < length
    pack_ref[...] = jnp.where(live, window, 0.0).astype(jnp.bfloat16)

    for copy in list(copies.values()) + parcels + sent:
        copy.wait_send()
    for g in range(n_g):
        for way in range(2):
            for step in range(n_hi - 1):
                pl.when(sends(way, step))(lambda g=g, way=way, step=step: line(g, way, step).wait_send())


def body(islands, tensor, pseudo_grad, outer_params, momentum, save_pages, writer):
    own_rows, col_width = outer_params.shape
    bits = islands.bit_length() - 1
    tiles = col_width // LANES
    page_count = own_rows * tiles
    capacity = 2 * page_count
    entries = islands * own_rows * col_width * tensor
    f32, bf16 = jnp.float32, jnp.bfloat16
    n_rs = len(cuts(page_count, 8, len(bit_orders(bits)) * ROUNDS))
    g_spans = cuts(page_count, 16, GATHER_CHUNKS)
    n_g = len(g_spans)
    n_lo = 1 << (bits // 2)
    n_hi = islands // n_lo
    dma = pltpu.SemaphoreType.DMA
    vmem = pl.BlockSpec(memory_space=pltpu.VMEM)
    smem = pl.BlockSpec(memory_space=pltpu.SMEM)

    def interleave(a):
        return a.reshape(-1, own_rows, tiles, LANES).swapaxes(1, 2).reshape(-1, page_count, LANES)

    def rows_of(a):
        return a.reshape(tiles, own_rows, LANES).swapaxes(0, 1).reshape(own_rows, col_width)

    x = pseudo_grad.reshape(-1, SUBLANES, tiles, LANES).swapaxes(1, 2)
    x = x.reshape(-1, tiles, SUBLANES // own_rows, own_rows, LANES).swapaxes(1, 2)
    x = x.reshape((2,) * bits + (page_count, LANES))
    master, moment, packed = pl.pallas_call(
        functools.partial(kernel, bits, tensor, own_rows, entries),
        out_shape=(
            jax.ShapeDtypeStruct((page_count, LANES), f32),
            jax.ShapeDtypeStruct((page_count, LANES), f32),
            jax.ShapeDtypeStruct((capacity, LANES), bf16),
        ),
        in_specs=[vmem] * 3 + [smem] * 2,
        out_specs=(vmem,) * 3,
        scratch_shapes=[pltpu.VMEM((2,) * (bits - s) + (page_count, LANES), f32) for s in range(1, bits + 1)]
        + [pltpu.VMEM((n_hi, size, LANES), bf16) for _, size in g_spans]
        + [pltpu.VMEM((n_lo, size, LANES), bf16) for _, size in g_spans]
        + [pltpu.VMEM((n_lo, size, LANES), bf16) for _, size in g_spans]
        + [
            pltpu.VMEM((page_count, LANES), f32),
            pltpu.VMEM((page_count, LANES), f32),
            pltpu.VMEM((capacity + page_count, LANES), f32),
            pltpu.VMEM((islands * tensor, 8, LANES), f32),
            dma((n_rs, bits)),
            dma((n_rs, bits)),
            dma((islands * tensor,)),
            dma((islands * tensor,)),
            dma((n_g, 2, n_hi)),
            dma((n_g, 2, n_hi)),
            dma((n_g, n_lo)),
            dma((n_g, n_lo)),
        ],
        compiler_params=pltpu.CompilerParams(collective_id=0, has_side_effects=True),
    )(x, interleave(outer_params)[0], interleave(momentum)[0], save_pages, writer)
    return rows_of(master), rows_of(moment), packed[None]


def solution(mesh):
    in_specs = (P("island", None, "tensor"), P("island", "tensor"), P("island", "tensor"), P(), P())
    out_specs = (P("island", "tensor"), P("island", "tensor"), P("island", None, "tensor"))
    step = functools.partial(body, mesh.shape["island"], mesh.shape["tensor"])
    return jax.shard_map(step, mesh=mesh, in_specs=in_specs, out_specs=out_specs, check_vma=False)
```

time: 87.8 us -> 81.3 us (0.926)
  other arithmetic: 3.33 us -> 0 us
  Pallas kernels: 72.7 us -> 69.5 us
  local copies, waits for them, and re-layouts: 8.78 us -> 10.9 us
  between operations: 2.75 us -> 0.64 us
    reshape x5 -> x0, local copies, waits for them, and re-layouts: 8.69 us -> none  [the longest x2 3.49 us: body(): return (master.reshape(shape), moment.reshape(shape), packed[None])]
    unnamed x8 -> x4, local copies, waits for them, and re-layouts: 0.02 us -> 7.45 us
    transpose x0 -> x1, local copies, waits for them, and re-layouts: none -> 3.49 us  [body(): x.reshape(-1, tiles, SUBLANES // own_rows, own_rows, LANES).swapaxes(1, 2)]
    pallas_call x1, Pallas kernels: 72.7 us -> 69.5 us  [body(): pl.pallas_call(functools.partial(kernel, bits, tensor, own_rows, entries)...]
    broadcast_in_dim x1 -> x0, other arithmetic: 1.81 us -> none  [body(): return (master.reshape(shape), moment.reshape(shape), packed[None])]
where the time goes in v2:
time: 81.3 us; the launch traced here: 81.1 us
  Pallas kernels  69.5 us (85%)
  local copies, waits for them, and re-layouts  10.9 us (13%)
    pallas_call x1, Pallas kernels, body(): pl.pallas_call(functools.partial(kernel, bits, tensor, own_rows, entries)...  69.5 us
    unnamed x4, local copies, waits for them, and re-layouts  7.45 us
    transpose x1, local copies, waits for them, and re-layouts, body(): x.reshape(-1, tiles, SUBLANES // own_rows, own_rows, LANES).swapaxes(1, 2)  3.49 us

profile of v2, /device:TPU:0, one launch (start us, length us, event | category | flops | bytes accessed | tf_op | source)
XLA Modules:
  0.0 81.1 jit_solution(3632809814774881243)
XLA Ops:
  0.6 2.6 %copy.19 = f32[4,8,208,128]{3,2,1,0:T(8,128)S(1)} copy(f32[4,8,208,128]{3,1,2,0:T(8,128)} %bitcast.35) | data formatting | bytes 6815744
  3.2 3.5 %copy.12 = f32[4,4,208,2,128]{4,3,2,1,0:T(2,128)} copy(f32[4,4,208,2,128]{4,2,3,1,0:T(8,128)S(1)} %bitcast.34) | data formatting | bytes 6815744 | tf_op jit(solution)/shard_map/transpose | solution.py:277
  6.7 69.5 %shard_map.76 = (f32[416,128]{1,0:T(8,128)}, f32[416,128]{1,0:T(8,128)}, bf16[832,128]{1,0:T(8,128)(2,1)}) custom-call(f32[2,2,2,2,416,128]{5,4,3,2,1,0:T(8,128)} %bitcast.33, f32[416,128]{1,0:T(8,128)} %bitcast.39, f32[416,128]{1,0:T(8,128)} %bitcast.40, s32[16]{0:T(128)} %refs_3_.1, s32[16]{0:T(128)} %refs_4_.1), custom_call_target="tpu_custom_call" | custom-call | tf_op jit(solution)/shard_map/pallas_call | solution.py:279
  76.2 1.6 %copy.23 = f32[2,26624]{1,0:T(2,128)} copy(f32[2,26624]{1,0:T(2,128)} %bitcast.38) | data formatting | bytes 425984
  77.8 1.6 %copy.24 = f32[2,26624]{1,0:T(2,128)} copy(f32[2,26624]{1,0:T(2,128)} %bitcast.37) | data formatting | bytes 425984
  79.4 1.6 %copy.25 = bf16[1,832,128]{2,1,0:T(8,128)(2,1)} copy(bf16[1,832,128]{2,1,0:T(8,128)(2,1)} %bitcast.36) | data formatting | bytes 425984

commit v3 on v2

--- a/solution.py
+++ b/solution.py
@@ -51,11 +51,13 @@
     capacity = pack_ref.shape[0]
     g_spans = cuts(page_count, 16, GATHER_CHUNKS)
     n_g = len(g_spans)
-    acc = [x_ref] + list(scratch[:bits])
-    held, parcel, landed = (scratch[bits + i * n_g : bits + (i + 1) * n_g] for i in range(3))
-    scratch = scratch[bits + 3 * n_g :]
+    raw, acc = scratch[0], scratch[1 : bits + 2]
+    scratch = scratch[1:]
+    scratch = scratch[bits + 1 :]
+    held, parcel, landed = (scratch[i * n_g : (i + 1) * n_g] for i in range(3))
+    scratch = scratch[3 * n_g :]
     sums, flat, span_buf, squares = scratch[:4]
-    rs_send, rs_recv, sq_send, sq_recv, line_send, line_recv, del_send, del_recv = scratch[4:]
+    rs_send, rs_recv, sq_send, sq_recv, line_send, line_recv, del_send, del_recv, in_sem = scratch[4:]
     islands = 1 << bits
     me = lax.axis_index("island")
     my_t = lax.axis_index("tensor")
@@ -71,13 +73,31 @@
     for k in range(1, islands * tensor):
         peers.append((k, {"island": flip(me, k // tensor, bits), "tensor": flip(my_t, k % tensor, t_bits)}))
 
+    orders = bit_orders(bits)
+    spans = cuts(page_count, SUBLANES, len(orders) * ROUNDS)
+    loads = []
+    for c, (low, size) in enumerate(spans):
+        part = pl.ds(low // rows * SUBLANES, size // rows * SUBLANES)
+        loads.append(pltpu.make_async_copy(x_ref.at[:, part, :], raw.at[:, part, :], in_sem.at[c]))
+        loads[c].start()
+
     barrier = pltpu.get_barrier_semaphore()
     for _, peer in peers:
         pl.semaphore_signal(barrier, inc=1, device_id=peer, device_id_type=MESH)
+
+    def lay_out(c):
+        low, size = spans[c]
+        loads[c].wait()
+        for i in range(islands):
+            group, first = i * rows // SUBLANES, i * rows % SUBLANES
+            for r in range(rows):
+                line = raw[group, pl.ds(low // rows * SUBLANES + first + r, size // rows, stride=SUBLANES), :]
+                to = tuple(i >> b & 1 for b in all_bits)
+                acc[0][to + (pl.ds(low + r, size // rows, stride=rows), slice(None))] = line
+
+    for c in range(len(orders)):
+        lay_out(c)
     pl.semaphore_wait(barrier, len(peers))
-
-    orders = bit_orders(bits)
-    spans = cuts(page_count, 8, len(orders) * ROUNDS)
 
     def left(c, s):
         used = orders[c % len(orders)][:s]
@@ -96,6 +116,8 @@
 
     copies = {}
     for c in range(len(spans)):
+        if c >= len(orders):
+            lay_out(c)
         copies[c, 1] = rs_copy(c, 1)
         copies[c, 1].start()
 
@@ -250,6 +272,11 @@
                 pl.when(sends(way, step))(lambda g=g, way=way, step=step: line(g, way, step).wait_send())
 
 
+def hand_on(*refs):
+    for source, target in zip(refs[:3], refs[3:]):
+        target[...] = source[...]
+
+
 def body(islands, tensor, pseudo_grad, outer_params, momentum, save_pages, writer):
     own_rows, col_width = outer_params.shape
     bits = islands.bit_length() - 1
@@ -258,7 +285,7 @@
     capacity = 2 * page_count
     entries = islands * own_rows * col_width * tensor
     f32, bf16 = jnp.float32, jnp.bfloat16
-    n_rs = len(cuts(page_count, 8, len(bit_orders(bits)) * ROUNDS))
+    n_rs = len(cuts(page_count, SUBLANES, len(bit_orders(bits)) * ROUNDS))
     g_spans = cuts(page_count, 16, GATHER_CHUNKS)
     n_g = len(g_spans)
     n_lo = 1 << (bits // 2)
@@ -274,8 +301,7 @@
         return a.reshape(tiles, own_rows, LANES).swapaxes(0, 1).reshape(own_rows, col_width)
 
     x = pseudo_grad.reshape(-1, SUBLANES, tiles, LANES).swapaxes(1, 2)
-    x = x.reshape(-1, tiles, SUBLANES // own_rows, own_rows, LANES).swapaxes(1, 2)
-    x = x.reshape((2,) * bits + (page_count, LANES))
+    x = x.reshape(-1, tiles * SUBLANES, LANES)
     master, moment, packed = pl.pallas_call(
         functools.partial(kernel, bits, tensor, own_rows, entries),
         out_shape=(
@@ -283,9 +309,10 @@
             jax.ShapeDtypeStruct((page_count, LANES), f32),
             jax.ShapeDtypeStruct((capacity, LANES), bf16),
         ),
-        in_specs=[vmem] * 3 + [smem] * 2,
+        in_specs=[pl.BlockSpec(memory_space=pl.ANY)] + [vmem] * 2 + [smem] * 2,
         out_specs=(vmem,) * 3,
-        scratch_shapes=[pltpu.VMEM((2,) * (bits - s) + (page_count, LANES), f32) for s in range(1, bits + 1)]
+        scratch_shapes=[pltpu.VMEM(x.shape, f32)]
+        + [pltpu.VMEM((2,) * (bits - s) + (page_count, LANES), f32) for s in range(bits + 1)]
         + [pltpu.VMEM((n_hi, size, LANES), bf16) for _, size in g_spans]
         + [pltpu.VMEM((n_lo, size, LANES), bf16) for _, size in g_spans]
         + [pltpu.VMEM((n_lo, size, LANES), bf16) for _, size in g_spans]
@@ -302,9 +329,16 @@
             dma((n_g, 2, n_hi)),
             dma((n_g, n_lo)),
             dma((n_g, n_lo)),
+            dma((n_rs,)),
         ],
         compiler_params=pltpu.CompilerParams(collective_id=0, has_side_effects=True),
     )(x, interleave(outer_params)[0], interleave(momentum)[0], save_pages, writer)
+    master, moment, packed = pl.pallas_call(
+        hand_on,
+        out_shape=tuple(jax.ShapeDtypeStruct(a.shape, a.dtype) for a in (master, moment, packed)),
+        in_specs=[vmem] * 3,
+        out_specs=(vmem,) * 3,
+    )(master, moment, packed)
     return rows_of(master), rows_of(moment), packed[None]
 
 

time: 81.3 us -> 71.3 us (0.88)
  local copies, waits for them, and re-layouts: 10.9 us -> 0 us
  Pallas kernels: 69.5 us -> 70.5 us
    unnamed x4 -> x0, local copies, waits for them, and re-layouts: 7.45 us -> none
    transpose x1 -> x0, local copies, waits for them, and re-layouts: 3.49 us -> none  [body(): x.reshape(-1, tiles, SUBLANES // own_rows, own_rows, LANES).swapaxes(1, 2)]
    pallas_call x0 -> x1, Pallas kernels: none -> 1.98 us  [body(): pl.pallas_call(hand_on, out_shape=tuple((jax.ShapeDtypeStruct(a.shape, a....]
    pallas_call x1, Pallas kernels: 69.5 us -> 68.5 us  [body(): pl.pallas_call(functools.partial(kernel, bits, tensor, own_rows, entries)...]
where the time goes in v3:
time: 71.3 us; the launch traced here: 71.1 us
  Pallas kernels  70.5 us (99%)
    pallas_call x1, Pallas kernels, body(): pl.pallas_call(functools.partial(kernel, bits, tensor, own_rows, entries)...  68.5 us
    pallas_call x1, Pallas kernels, body(): pl.pallas_call(hand_on, out_shape=tuple((jax.ShapeDtypeStruct(a.shape, a....  1.98 us

profile of v3, /device:TPU:0, one launch (start us, length us, event | category | flops | bytes accessed | tf_op | source)
XLA Modules:
  0.0 71.1 jit_solution(16723935038528373302)
XLA Ops:
  0.6 68.5 %shard_map.76 = (f32[416,128]{1,0:T(8,128)}, f32[416,128]{1,0:T(8,128)}, bf16[832,128]{1,0:T(8,128)(2,1)}) custom-call(f32[4,1664,128]{2,1,0:T(8,128)} %bitcast.26, f32[416,128]{1,0:T(8,128)} %bitcast.27, f32[416,128]{1,0:T(8,128)} %bitcast.28, s32[16]{0:T(128)} %refs_3_.1, s32[16]{0:T(128)} %refs_4_.1), custom_call_target="tpu_custom_call" | custom-call | tf_op jit(solution)/shard_map/pallas_call | solution.py:305
  69.2 2.0 %shard_map.77 = (f32[416,128]{1,0:T(8,128)}, f32[416,128]{1,0:T(8,128)}, bf16[832,128]{1,0:T(8,128)(2,1)}) custom-call(f32[416,128]{1,0:T(8,128)} %get-tuple-element.9.refs_0_, f32[416,128]{1,0:T(8,128)} %get-tuple-element.10.refs_1_, bf16[832,128]{1,0:T(8,128)(2,1)} %get-tuple-element.11.refs_2_), custom_call_target="tpu_custom_call" | custom-call | tf_op jit(solution)/shard_map/pallas_call | solution.py:336

commit v4 on v3

--- a/solution.py
+++ b/solution.py
@@ -12,7 +12,7 @@
 outer_rate = 0.7
 LANES = 128
 SUBLANES = 8
-ROUNDS = 3
+ROUNDS = 2
 GATHER_CHUNKS = 2
 MESH = pl.DeviceIdType.MESH
 
@@ -29,7 +29,9 @@
     orders = []
     for lead in range(min(3, bits)):
         orders.append([lead] + [b for b in base if b != lead])
-    return orders
+    if bits < 3:
+        return orders
+    return orders + orders[:2] + [[2, 1, 0] + base[3:]]
 
 
 def at(bits_left, fixed, span):
@@ -95,7 +97,7 @@
                 to = tuple(i >> b & 1 for b in all_bits)
                 acc[0][to + (pl.ds(low + r, size // rows, stride=rows), slice(None))] = line
 
-    for c in range(len(orders)):
+    for c in range(3):
         lay_out(c)
     pl.semaphore_wait(barrier, len(peers))
 
@@ -116,14 +118,14 @@
 
     copies = {}
     for c in range(len(spans)):
-        if c >= len(orders):
+        if c >= 3:
             lay_out(c)
         copies[c, 1] = rs_copy(c, 1)
         copies[c, 1].start()
 
     def when(item):
         c, s = item
-        r = c // len(orders)
+        r = c // 3 * 0.75
         return (0.1 * r if s == 1 else 1.1 * s + r, c)
 
     steps = sorted(((c, s) for c in range(len(spans)) for s in range(1, bits + 1)), key=when)

time: 71.3 us -> 71.5 us (level)
  no operation moved by 1% of the time
where the time goes in v4:
time: 71.5 us; the launch traced here: 71.4 us
  Pallas kernels  70.7 us (99%)
    pallas_call x1, Pallas kernels, body(): pl.pallas_call(functools.partial(kernel, bits, tensor, own_rows, entries)...  68.8 us
    pallas_call x1, Pallas kernels, body(): pl.pallas_call(hand_on, out_shape=tuple((jax.ShapeDtypeStruct(a.shape, a....  1.98 us

profile of v4, /device:TPU:0, one launch (start us, length us, event | category | flops | bytes accessed | tf_op | source)
XLA Modules:
  0.0 71.4 jit_solution(3235853391776800532)
XLA Ops:
  0.6 68.8 %shard_map.76 = (f32[416,128]{1,0:T(8,128)}, f32[416,128]{1,0:T(8,128)}, bf16[832,128]{1,0:T(8,128)(2,1)}) custom-call(f32[4,1664,128]{2,1,0:T(8,128)} %bitcast.26, f32[416,128]{1,0:T(8,128)} %bitcast.27, f32[416,128]{1,0:T(8,128)} %bitcast.28, s32[16]{0:T(128)} %refs_3_.1, s32[16]{0:T(128)} %refs_4_.1), custom_call_target="tpu_custom_call" | custom-call | tf_op jit(solution)/shard_map/pallas_call | solution.py:307
  69.4 2.0 %shard_map.77 = (f32[416,128]{1,0:T(8,128)}, f32[416,128]{1,0:T(8,128)}, bf16[832,128]{1,0:T(8,128)(2,1)}) custom-call(f32[416,128]{1,0:T(8,128)} %get-tuple-element.9.refs_0_, f32[416,128]{1,0:T(8,128)} %get-tuple-element.10.refs_1_, bf16[832,128]{1,0:T(8,128)(2,1)} %get-tuple-element.11.refs_2_), custom_call_target="tpu_custom_call" | custom-call | tf_op jit(solution)/shard_map/pallas_call | solution.py:338
